TPU v7x, 32 devices: a whole 2x2x4 slice. The times are simulated.
32 devices in a mesh: tm: 16 (over z, y, core), asset: 2 (over x).
Axes of the slice: x: 2, y: 2, z: 4, core: 2. Of those that a mesh axis runs over, the one named last changes fastest.
Arguments:
- tick_bars: float32 [2, 16, 61440], P('asset', 'tm'), may hold values from -20 to 20
- prior_bars: float32 [2, 16, 6400], P('asset', 'tm'), may hold values from -20 to 20, as said below
Outputs:
- connectedness: float32 [48, 8192], P('tm', 'asset')
Inputs may be any that keep to these rules, and one draw needn't show every extreme that they name: `prior_bars`: bar returns of the same assets.
All inputs are finite; a program needn't handle non-finite values.
Results may differ from a plain program's by a relative error of at most 0.0014.
Values may be sent and summed in bfloat16 or wider, within the bound.
A program may use at most 64 MiB of HBM per device.

v0:
```python
import math
import jax
import jax.numpy as jnp
from jax import lax
from jax.sharding import PartitionSpec as P

ASSETS = 8192
SPAN = 30
STRIDE = 5
WIN_DEV = 3
LEAD = 25
FLOOR_SQUARES = 1.0


def from_behind(x, axis, by):
    size = lax.axis_size(axis)
    pairs = [(i, i + by) for i in range(size) if 0 <= i + by < size]
    return lax.ppermute(x, axis, pairs)


def swapped(block, axis, distance):
    count = lax.axis_size(axis)
    route = []
    for low in range(count):
        high = low | 1 << distance
        if high != low and high < count:
            route += [(low, high), (high, low)]
    return lax.ppermute(block, axis, route)


def window_stack(extended):
    columns = extended.shape[1]
    groups = extended.reshape(-1, STRIDE, columns)
    stacked = jnp.stack(
        [groups[offset : offset + WIN_DEV] for offset in range(SPAN // STRIDE)], axis=1
    )
    values = stacked.reshape(WIN_DEV, SPAN, columns)
    centred = values - jnp.mean(values, axis=1, keepdims=True)
    squares = jnp.sum(centred * centred, axis=1, keepdims=True)
    return (centred * lax.rsqrt(jnp.maximum(squares, FLOOR_SQUARES))).astype(jnp.bfloat16)


def block_magnitude(left_part, right_part, offset, block_rows):
    correlation = lax.dot_general(
        left_part[:, offset : offset + block_rows],
        right_part,
        (((0,), (0,)), ((), ())),
        preferred_element_type=jnp.float32,
    )
    return jnp.abs(correlation.astype(jnp.bfloat16)).astype(jnp.float32)


def row_totals(own_windows, other_windows):
    columns = own_windows.shape[2]
    block_rows = min(1024, columns)

    def row_one_window(operands):
        left_part, right_part = operands
        pieces = [
            jnp.sum(block_magnitude(left_part, right_part, offset, block_rows), axis=1)
            for offset in range(0, columns, block_rows)
        ]
        return jnp.concatenate(pieces)

    return lax.map(row_one_window, (own_windows, other_windows))


def both_totals(own_windows, other_windows):
    columns = own_windows.shape[2]
    block_rows = min(1024, columns)

    def both_one_window(operands):
        left_part, right_part = operands
        pieces = []
        column_total = jnp.zeros((right_part.shape[1],), jnp.float32)
        for offset in range(0, columns, block_rows):
            magnitude = block_magnitude(left_part, right_part, offset, block_rows)
            pieces.append(jnp.sum(magnitude, axis=1))
            column_total = column_total + jnp.sum(magnitude, axis=0)
        return (jnp.concatenate(pieces), column_total)

    return lax.map(both_one_window, (own_windows, other_windows))


def earlier_rows(tail_rows, distance):
    return from_behind(tail_rows, "tm", distance)


def time_block_rows(tick_bars, prior_bars):
    groups = lax.axis_size("tm")
    group_cols = ASSETS // (2 * groups)
    outgoing = tick_bars.reshape(groups, 1, -1)
    arrived = lax.all_to_all(outgoing, "tm", split_axis=0, concat_axis=1, tiled=True)
    block_len = arrived.shape[2] // group_cols
    own_rows = jnp.transpose(arrived.reshape(groups, block_len, group_cols), (1, 0, 2)).reshape(
        block_len, groups * group_cols
    )
    prior_all = lax.all_gather(prior_bars, "tm", axis=1, tiled=True)
    series_prior = jnp.transpose(prior_all.reshape(groups, LEAD, group_cols), (1, 0, 2)).reshape(
        LEAD, groups * group_cols
    )
    reach = (LEAD + block_len - 1) // block_len
    earlier = []
    for distance in range(reach, 0, -1):
        needed = min(block_len, LEAD - (distance - 1) * block_len)
        earlier.append(earlier_rows(own_rows[block_len - needed :], distance))
    history = jnp.concatenate(earlier, axis=0)
    position = lax.axis_index("tm")
    first_row = position * block_len
    padded = jnp.concatenate([series_prior, jnp.zeros_like(series_prior)], axis=0)
    from_prior = lax.dynamic_slice_in_dim(padded, jnp.minimum(first_row, LEAD), LEAD, 0)
    before_start = first_row - LEAD + jnp.arange(LEAD, dtype=jnp.int32) < 0
    history = jnp.where(before_start[:, None], from_prior, history)
    return jnp.concatenate([history, own_rows], axis=0)


def shards(tick_bars, prior_bars):
    extended = time_block_rows(tick_bars, prior_bars)
    scaled = window_stack(extended)
    columns = scaled.shape[2]
    empty = jnp.zeros((WIN_DEV, columns), jnp.float32)
    partner = swapped(scaled, "asset", 0)
    tile_index = lax.axis_index("asset")
    quarter = columns // 2
    diagonal_part = row_totals(scaled, scaled)
    column_part = empty
    cross_rows = []
    for half_index in range(2):
        mine = scaled[:, :, half_index * quarter : (half_index + 1) * quarter]
        target = (half_index + tile_index) % 2
        theirs = lax.dynamic_slice_in_dim(partner, target * quarter, quarter, 2)
        row_add, column_add = both_totals(mine, theirs)
        cross_rows.append(row_add)
        column_part = lax.dynamic_update_slice_in_dim(column_part, column_add, target * quarter, 1)
    returned = swapped(column_part.astype(jnp.bfloat16), "asset", 0).astype(column_part.dtype)
    totals = diagonal_part + jnp.concatenate(cross_rows, axis=1) + returned
    return totals * (math.sqrt(SPAN) / ASSETS)


def solution(mesh):
    in_specs = (P("asset", "tm", None), P("asset", "tm", None))
    out_specs = P("tm", "asset")
    return jax.shard_map(shards, mesh=mesh, in_specs=in_specs, out_specs=out_specs, check_vma=False)
```

profile of v0, /device:TPU:0, one launch (start us, length us, event | category | flops | bytes accessed | tf_op | source)
XLA Modules:
  0.0 132.5 jit_solution(15997069284028944891)
XLA Ops:
  0.0 7.5 %all-to-all-start = ((f32[16,1,3840]{2,1,0:T(1,128)}), f32[16,1,3840]{2,1,0:T(1,128)S(1)}, u32[]{:S(2)}, u32[]{:S(2)}) async-start(f32[16,1,3840]{2,1,0:T(1,128)} %bitcast.93), calls=%async_computation | async-start | bytes 491520 | tf_op jit(solution)/shard_map/all_to_all | solution.py:93
  7.6 9.8 %all-to-all-done = f32[16,1,3840]{2,1,0:T(1,128)S(1)} async-done(((f32[16,1,3840]{2,1,0:T(1,128)}), f32[16,1,3840]{2,1,0:T(1,128)S(1)}, u32[]{:S(2)}, u32[]{:S(2)}) %all-to-all-start) | async-done | bytes 245792 | tf_op jit(solution)/shard_map/all_to_all | solution.py:93
  18.3 1.8 %collective-permute-start.1 = (f32[15,4096]{1,0:T(8,128)S(1)}, f32[15,4096]{1,0:T(8,128)S(1)}, u32[]{:S(2)}, u32[]{:S(2)}) collective-permute-start(f32[15,4096]{1,0:T(8,128)S(1)} %bitcast.86), channel_id=1, source_target_pairs={{0,2},{2,4},{4,6},{6,8},{8,10},{10,12},{12,14},{14,16},{16,18},{18... | collective-permute-start | bytes 737288 | tf_op jit(solution)/shard_map/ppermute | solution.py:18
  20.4 2.5 %collective-permute-start = (f32[10,4096]{1,0:T(8,128)S(1)}, f32[10,4096]{1,0:T(8,128)S(1)}, u32[]{:S(2)}, u32[]{:S(2)}) collective-permute-start(f32[10,4096]{1,0:T(8,128)S(1)} %bitcast.92), channel_id=1, source_target_pairs={{0,4},{2,6},{4,8},{6,10},{8,12},{10,14},{12,16},{14,18},{16,20},{1... | collective-permute-start | bytes 491528 | tf_op jit(solution)/shard_map/ppermute | solution.py:18
  23.0 22.3 %all_gather.3 = f32[1,16,6400]{2,0,1:T(1,128)S(1)} all-gather(f32[1,1,6400]{2,0,1:T(1,128)S(1)} %bitcast.94), channel_id=1, replica_groups=mesh['tm'=16,'asset'=2] {'tm'}, dimensions={1}, use_global_device_ids=true | all-gather | bytes 435200 | tf_op jit(solution)/shard_map/all_gather | solution.py:98
  49.1 1.7 %stack.22 = f32[3,1,5,4096]{3,2,0,1:T(8,128)} reshape(f32[15,4096]{1,0:T(8,128)} %get-tuple-element.124) | data formatting | bytes 491520 | tf_op jit(solution)/shard_map/stack | solution.py:34
  50.8 1.7 %stack.23 = f32[3,1,5,4096]{3,2,0,1:T(8,128)} reshape(f32[15,4096]{1,0:T(8,128)} %get-tuple-element.123) | data formatting | bytes 491520 | tf_op jit(solution)/shard_map/stack | solution.py:34
  59.4 1.7 %reshape.86 = f32[3,30,4096]{2,1,0:T(8,128)S(1)} reshape(f32[3,6,5,4096]{3,2,1,0:T(8,128)} %copy.14) | data formatting | bytes 2949120 | tf_op jit(solution)/shard_map/reshape | solution.py:37
  62.9 18.2 %collective-permute-done.2 = bf16[3,30,4096]{2,1,0:T(8,128)(2,1)S(1)} collective-permute-done((bf16[3,30,4096]{2,1,0:T(8,128)(2,1)S(1)}, bf16[3,30,4096]{2,1,0:T(8,128)(2,1)S(1)}, u32[]{:S(2)}, u32[]{:S(2)}) %collective-permute-start.2) | collective-permute-done | bytes 737312 | tf_op jit(solution)/shard_map/ppermute | solution.py:28
  81.3 9.1 %while.35 = (s32[]{:T(128)}, f32[3,2048]{1,0:T(4,128)S(1)}, f32[3,2048]{1,0:T(4,128)S(1)}, bf16[3,30,2048]{2,1,0:T(8,128)(2,1)S(1)}, bf16[3,30,2048]{2,1,0:T(8,128)(2,1)S(1)}, /*index=5*/s32[]{:T(128)}, s32[]{:T(128)}) while((s32[]{:T(128)}, f32[3,2048]{1,0:T(4,128)S(1)}, f32[3,2048]{1,0:T(4,128)S(1)}, bf16[3,30,2048]{2,1,0:T(8,128)(2,1)S(1)}, ...), condition=%wide.region_18.19_spmd, body=%wide.region_13.18_spmd.sunk | while | flops 272627712 | bytes 737377 | solution.py:82
  90.4 9.2 %while.36 = (s32[]{:T(128)}, f32[3,2048]{1,0:T(4,128)S(1)}, f32[3,2048]{1,0:T(4,128)S(1)}, bf16[3,30,2048]{2,1,0:T(8,128)(2,1)S(1)}, bf16[3,30,2048]{2,1,0:T(8,128)(2,1)S(1)}, /*index=5*/s32[]{:T(128)}, s32[]{:T(128)}) while((s32[]{:T(128)}, f32[3,2048]{1,0:T(4,128)S(1)}, f32[3,2048]{1,0:T(4,128)S(1)}, bf16[3,30,2048]{2,1,0:T(8,128)(2,1)S(1)}, ...), condition=%wide.region_24.25_spmd, body=%wide.region_19.24_spmd.sunk | while | flops 272627712 | bytes 737377 | solution.py:82
  101.3 30.5 %while.34 = (s32[]{:T(128)}, f32[3,4096]{1,0:T(4,128)S(1)}, bf16[3,30,4096]{2,1,0:T(8,128)(2,1)S(1)}, s32[]{:T(128)}, s32[]{:T(128)}) while((s32[]{:T(128)}, f32[3,4096]{1,0:T(4,128)S(1)}, bf16[3,30,4096]{2,1,0:T(8,128)(2,1)S(1)}, s32[]{:T(128)}, s32[]{:T(128)}) %tuple.68), condition=%wide.region_12.13_spmd, body=%wide.region_7.12_spmd.sunk | while | flops 1073750016 | bytes 1884229 | solution.py:65
  101.5 2.4 %convert_reduce_fusion.20 = f32[1024]{0:T(1024)S(1)} fusion(bf16[30,4096]{1,0:T(8,128)(2,1)S(1)} %dynamic-slice_bitcast_fusion.6), kind=kOutput, calls=%fused_computation.clone.1 | convolution fusion | flops 268434432 | bytes 331776 | tf_op jit(solution)/shard_map/while/body/eval_jaxpr/dot_general | solution.py:44
  104.0 2.5 %convert_reduce_fusion.21 = f32[1024]{0:T(1024)S(1)} fusion(bf16[30,4096]{1,0:T(8,128)(2,1)S(1)} %dynamic-slice_bitcast_fusion.6), kind=kOutput, calls=%fused_computation.1.clone.1 | convolution fusion | flops 268434432 | bytes 331776 | tf_op jit(solution)/shard_map/while/body/eval_jaxpr/dot_general | solution.py:44
  106.4 2.5 %convert_reduce_fusion.22 = f32[1024]{0:T(1024)S(1)} fusion(bf16[30,4096]{1,0:T(8,128)(2,1)S(1)} %dynamic-slice_bitcast_fusion.6), kind=kOutput, calls=%fused_computation.2.clone.1 | convolution fusion | flops 268434432 | bytes 331776 | tf_op jit(solution)/shard_map/while/body/eval_jaxpr/dot_general | solution.py:44
  108.9 2.5 %convert_reduce_fusion.23 = f32[1024]{0:T(1024)S(1)} fusion(bf16[30,4096]{1,0:T(8,128)(2,1)S(1)} %dynamic-slice_bitcast_fusion.6), kind=kOutput, calls=%fused_computation.3.clone.1 | convolution fusion | flops 268434432 | bytes 331776 | tf_op jit(solution)/shard_map/while/body/eval_jaxpr/dot_general | solution.py:44
  111.6 2.4 %convert_reduce_fusion.20 = f32[1024]{0:T(1024)S(1)} fusion(bf16[30,4096]{1,0:T(8,128)(2,1)S(1)} %dynamic-slice_bitcast_fusion.6), kind=kOutput, calls=%fused_computation.clone.1 | convolution fusion | flops 268434432 | bytes 331776 | tf_op jit(solution)/shard_map/while/body/eval_jaxpr/dot_general | solution.py:44
  114.1 2.5 %convert_reduce_fusion.21 = f32[1024]{0:T(1024)S(1)} fusion(bf16[30,4096]{1,0:T(8,128)(2,1)S(1)} %dynamic-slice_bitcast_fusion.6), kind=kOutput, calls=%fused_computation.1.clone.1 | convolution fusion | flops 268434432 | bytes 331776 | tf_op jit(solution)/shard_map/while/body/eval_jaxpr/dot_general | solution.py:44
  116.5 2.5 %convert_reduce_fusion.22 = f32[1024]{0:T(1024)S(1)} fusion(bf16[30,4096]{1,0:T(8,128)(2,1)S(1)} %dynamic-slice_bitcast_fusion.6), kind=kOutput, calls=%fused_computation.2.clone.1 | convolution fusion | flops 268434432 | bytes 331776 | tf_op jit(solution)/shard_map/while/body/eval_jaxpr/dot_general | solution.py:44
  119.0 2.5 %convert_reduce_fusion.23 = f32[1024]{0:T(1024)S(1)} fusion(bf16[30,4096]{1,0:T(8,128)(2,1)S(1)} %dynamic-slice_bitcast_fusion.6), kind=kOutput, calls=%fused_computation.3.clone.1 | convolution fusion | flops 268434432 | bytes 331776 | tf_op jit(solution)/shard_map/while/body/eval_jaxpr/dot_general | solution.py:44
  121.7 2.4 %convert_reduce_fusion.20 = f32[1024]{0:T(1024)S(1)} fusion(bf16[30,4096]{1,0:T(8,128)(2,1)S(1)} %dynamic-slice_bitcast_fusion.6), kind=kOutput, calls=%fused_computation.clone.1 | convolution fusion | flops 268434432 | bytes 331776 | tf_op jit(solution)/shard_map/while/body/eval_jaxpr/dot_general | solution.py:44
  124.2 2.5 %convert_reduce_fusion.21 = f32[1024]{0:T(1024)S(1)} fusion(bf16[30,4096]{1,0:T(8,128)(2,1)S(1)} %dynamic-slice_bitcast_fusion.6), kind=kOutput, calls=%fused_computation.1.clone.1 | convolution fusion | flops 268434432 | bytes 331776 | tf_op jit(solution)/shard_map/while/body/eval_jaxpr/dot_general | solution.py:44
  126.6 2.5 %convert_reduce_fusion.22 = f32[1024]{0:T(1024)S(1)} fusion(bf16[30,4096]{1,0:T(8,128)(2,1)S(1)} %dynamic-slice_bitcast_fusion.6), kind=kOutput, calls=%fused_computation.2.clone.1 | convolution fusion | flops 268434432 | bytes 331776 | tf_op jit(solution)/shard_map/while/body/eval_jaxpr/dot_general | solution.py:44
  129.1 2.5 %convert_reduce_fusion.23 = f32[1024]{0:T(1024)S(1)} fusion(bf16[30,4096]{1,0:T(8,128)(2,1)S(1)} %dynamic-slice_bitcast_fusion.6), kind=kOutput, calls=%fused_computation.3.clone.1 | convolution fusion | flops 268434432 | bytes 331776 | tf_op jit(solution)/shard_map/while/body/eval_jaxpr/dot_general | solution.py:44
  (104 shorter events, 34.8 us)
Async XLA Ops:
  0.0 23.0 %copy-start.1 = (f32[1,1,6400]{2,1,0:T(1,128)S(1)}, f32[1,1,6400]{2,1,0:T(1,128)}, u32[]{:S(2)}) copy-start(f32[1,1,6400]{2,1,0:T(1,128)} %param.9) | copy-start | bytes 76804
  0.0 17.3 %all-to-all-start = ((f32[16,1,3840]{2,1,0:T(1,128)}), f32[16,1,3840]{2,1,0:T(1,128)S(1)}, u32[]{:S(2)}, u32[]{:S(2)}) async-start(f32[16,1,3840]{2,1,0:T(1,128)} %bitcast.93), calls=%async_computation | async-start | bytes 491520 | tf_op jit(solution)/shard_map/all_to_all | solution.py:93
  18.3 28.7 %collective-permute-start.1 = (f32[15,4096]{1,0:T(8,128)S(1)}, f32[15,4096]{1,0:T(8,128)S(1)}, u32[]{:S(2)}, u32[]{:S(2)}) collective-permute-start(f32[15,4096]{1,0:T(8,128)S(1)} %bitcast.86), channel_id=1, source_target_pairs={{0,2},{2,4},{4,6},{6,8},{8,10},{10,12},{12,14},{14,16},{16,18},{18... | collective-permute-start | bytes 737288 | tf_op jit(solution)/shard_map/ppermute | solution.py:18
  20.4 26.6 %collective-permute-start = (f32[10,4096]{1,0:T(8,128)S(1)}, f32[10,4096]{1,0:T(8,128)S(1)}, u32[]{:S(2)}, u32[]{:S(2)}) collective-permute-start(f32[10,4096]{1,0:T(8,128)S(1)} %bitcast.92), channel_id=1, source_target_pairs={{0,4},{2,6},{4,8},{6,10},{8,12},{10,14},{12,16},{14,18},{16,20},{1... | collective-permute-start | bytes 491528 | tf_op jit(solution)/shard_map/ppermute | solution.py:18
  57.3 1.6 %copy-start = (f32[3,4096]{1,0:T(4,128)S(1)}, f32[3,4096]{1,0:T(4,128)}, u32[]{:S(2)}) copy-start(f32[3,4096]{1,0:T(4,128)} %get-tuple-element.128) | copy-start | bytes 147460
  61.3 19.9 %collective-permute-start.2 = (bf16[3,30,4096]{2,1,0:T(8,128)(2,1)S(1)}, bf16[3,30,4096]{2,1,0:T(8,128)(2,1)S(1)}, u32[]{:S(2)}, u32[]{:S(2)}) collective-permute-start(bf16[3,30,4096]{2,1,0:T(8,128)(2,1)S(1)} %multiply_convert_fusion), channel_id=1, source_target_pairs={{0,1},{1,0},{2,3},{3,2},{4,5},{5,4},{6,7},{7,6},{8,9},{9,8},{10,11... | collective-permute-start | bytes 2211848 | tf_op jit(solution)/shard_map/ppermute | solution.py:28
  99.7 32.1 %collective-permute-start.3 = (bf16[3,4096]{1,0:T(4,128)(2,1)S(1)}, bf16[3,4096]{1,0:T(4,128)(2,1)S(1)}, u32[]{:S(2)}, u32[]{:S(2)}) collective-permute-start(bf16[3,4096]{1,0:T(4,128)(2,1)S(1)} %convert_element_type.58), channel_id=1, source_target_pairs={{0,1},{1,0},{2,3},{3,2},{4,5},{5,4},{6,7},{7,6},{8,9},{9,8},{10,11... | collective-permute-start | bytes 73736 | tf_op jit(solution)/shard_map/ppermute | solution.py:28
where the time goes:
time: 133 us; the launch traced here: 132 us
  matrix products  45.7 us (34%)
  waiting for transfers between devices  28 us (21%)
  blocking collectives  22.3 us (17%)
  starting transfers between devices  15 us (11%)
  local copies, waits for them, and re-layouts  12.9 us (10%)
  other arithmetic  7.66 us (6%)
    dot_general x24, matrix products, block_magnitude(): lax.dot_general(left_part[:, offset:offset + block_rows], right_part, (((...  45.7 us
    all_gather x1, blocking collectives, time_block_rows(): prior_all = lax.all_gather(prior_bars, 'tm', axis=1, tiled=True)  22.3 us
    ppermute x2, waiting for transfers between devices, swapped(): return lax.ppermute(block, axis, route)  18.2 us
    all_to_all x1, waiting for transfers between devices, time_block_rows(): lax.all_to_all(outgoing, 'tm', split_axis=0, concat_axis=1, tiled=True)  9.75 us
    all_to_all x1, starting transfers between devices, time_block_rows(): lax.all_to_all(outgoing, 'tm', split_axis=0, concat_axis=1, tiled=True)  7.55 us
    another operation x7, local copies, waits for them, and re-layouts, window_stack(): jnp.stack([groups[offset:offset + WIN_DEV] for offset in range(SPAN // ST...  7.1 us
    ppermute x2, starting transfers between devices, from_behind(): return lax.ppermute(x, axis, pairs)  4.3 us
    reduce_sum x6, other arithmetic, window_stack(): centred = values - jnp.mean(values, axis=1, keepdims=True)  3.52 us
  transfers between devices with their start and end apart: 5, of which 2 were waited for; matrix products, arithmetic and copies ran while one was open for 24% of the time, Pallas kernels for 0%

commit v1 on v0

--- a/solution.py
+++ b/solution.py
@@ -95,7 +95,22 @@
     own_rows = jnp.transpose(arrived.reshape(groups, block_len, group_cols), (1, 0, 2)).reshape(
         block_len, groups * group_cols
     )
-    prior_all = lax.all_gather(prior_bars, "tm", axis=1, tiled=True)
+    ways, here, step = (lax.axis_size("tm"), lax.axis_index("tm"), prior_bars.shape[1])
+    lengths = [n * ways if d == 1 else n for d, n in enumerate(prior_bars.shape)]
+    prior_all = lax.dynamic_update_slice_in_dim(
+        jnp.zeros(lengths, prior_bars.dtype), prior_bars, here * step, axis=1
+    )
+    going_up = going_down = prior_bars
+    for far in range(1, ways // 2 + 1):
+        going_up = lax.ppermute(going_up, "tm", [(d, (d + 1) % ways) for d in range(ways)])
+        prior_all = lax.dynamic_update_slice_in_dim(
+            prior_all, going_up, (here - far) % ways * step, axis=1
+        )
+        if 2 * far < ways:
+            going_down = lax.ppermute(going_down, "tm", [(d, (d - 1) % ways) for d in range(ways)])
+            prior_all = lax.dynamic_update_slice_in_dim(
+                prior_all, going_down, (here + far) % ways * step, axis=1
+            )
     series_prior = jnp.transpose(prior_all.reshape(groups, LEAD, group_cols), (1, 0, 2)).reshape(
         LEAD, groups * group_cols
     )

time: 133 us -> 146 us (1.098)
  starting transfers between devices: 15 us -> 44.5 us
  blocking collectives: 22.3 us -> 0 us
  local copies, waits for them, and re-layouts: 12.9 us -> 21.9 us
  waiting for transfers between devices: 28 us -> 25.2 us
    ppermute x0 -> x15, starting transfers between devices: none -> 31.3 us  [the longest x7 30.9 us: time_block_rows(): lax.ppermute(going_down, 'tm', [(d, (d - 1) % ways) for d in range(ways)])]
    all_gather x1 -> x0, blocking collectives: 22.3 us -> none  [time_block_rows(): prior_all = lax.all_gather(prior_bars, 'tm', axis=1, tiled=True)]
    ppermute x0 -> x15, waiting for transfers between devices: none -> 11.4 us  [the longest x8 6.78 us: time_block_rows(): lax.ppermute(going_up, 'tm', [(d, (d + 1) % ways) for d in range(ways)])]
    dynamic_update_slice x0 -> x16, local copies, waits for them, and re-layouts: none -> 9.97 us  [the longest x8 5.07 us: time_block_rows(): lax.dynamic_update_slice_in_dim(prior_all, going_up, (here - far) % ways...]
    all_to_all x1, waiting for transfers between devices: 9.75 us -> 0.01 us  [time_block_rows(): lax.all_to_all(outgoing, 'tm', split_axis=0, concat_axis=1, tiled=True)]
    ppermute x2, waiting for transfers between devices: 18.2 us -> 13.9 us  [swapped(): return lax.ppermute(block, axis, route)]
    ppermute x2, starting transfers between devices: 4.3 us -> 2.61 us  [from_behind(): return lax.ppermute(x, axis, pairs)]
  transfers between devices with their start and end apart: 5 -> 20, of which waited for: 2 -> 6; matrix products, arithmetic and copies ran while one was open for 24% -> 29% of each run, Pallas kernels for 0% -> 0%
where the time goes in v1:
time: 146 us; the launch traced here: 145 us
  matrix products  45.7 us (31%)
  starting transfers between devices  44.5 us (30%)
  waiting for transfers between devices  25.2 us (17%)
  local copies, waits for them, and re-layouts  21.9 us (15%)
  other arithmetic  6.6 us (5%)
    dot_general x24, matrix products, block_magnitude(): lax.dot_general(left_part[:, offset:offset + block_rows], right_part, (((...  45.7 us
    ppermute x7, starting transfers between devices, time_block_rows(): lax.ppermute(going_down, 'tm', [(d, (d - 1) % ways) for d in range(ways)])  30.9 us
    ppermute x2, waiting for transfers between devices, swapped(): return lax.ppermute(block, axis, route)  13.9 us
    all_to_all x1, starting transfers between devices, time_block_rows(): lax.all_to_all(outgoing, 'tm', split_axis=0, concat_axis=1, tiled=True)  7.41 us
    ppermute x8, waiting for transfers between devices, time_block_rows(): lax.ppermute(going_up, 'tm', [(d, (d + 1) % ways) for d in range(ways)])  6.78 us
    another operation x7, local copies, waits for them, and re-layouts, window_stack(): jnp.stack([groups[offset:offset + WIN_DEV] for offset in range(SPAN // ST...  6.15 us
    dynamic_update_slice x8, local copies, waits for them, and re-layouts, time_block_rows(): lax.dynamic_update_slice_in_dim(prior_all, going_up, (here - far) % ways...  5.07 us
    ppermute x7, waiting for transfers between devices, time_block_rows(): lax.ppermute(going_down, 'tm', [(d, (d - 1) % ways) for d in range(ways)])  4.58 us
  transfers between devices with their start and end apart: 20, of which 6 were waited for; matrix products, arithmetic and copies ran while one was open for 29% of the time, Pallas kernels for 0%

profile of v1, /device:TPU:0, one launch (start us, length us, event | category | flops | bytes accessed | tf_op | source)
XLA Modules:
  0.0 145.4 jit_solution(11642380642806564775)
XLA Ops:
  0.0 7.4 %all-to-all-start = ((f32[16,1,3840]{2,1,0:T(1,128)}), f32[16,1,3840]{2,1,0:T(1,128)S(1)}, u32[]{:S(2)}, u32[]{:S(2)}) async-start(f32[16,1,3840]{2,1,0:T(1,128)} %bitcast.92), calls=%async_computation | async-start | bytes 491520 | tf_op jit(solution)/shard_map/all_to_all | solution.py:93
  7.8 4.1 %collective-permute-start.1 = (f32[1,1,6400]{2,1,0:T(1,128)}, f32[1,1,6400]{2,1,0:T(1,128)S(1)}, u32[]{:S(2)}, u32[]{:S(2)}) collective-permute-start(f32[1,1,6400]{2,1,0:T(1,128)} %param.9), channel_id=1, source_target_pairs={{0,30},{2,0},{4,2},{6,4},{8,6},{10,8},{12,10},{14,12},{16,14},{18,... | collective-permute-start | bytes 76808 | tf_op jit(solution)/shard_map/ppermute | solution.py:110
  11.9 5.2 %collective-permute-done = f32[1,1,6400]{2,1,0:T(1,128)S(1)} collective-permute-done((f32[1,1,6400]{2,1,0:T(1,128)}, f32[1,1,6400]{2,1,0:T(1,128)S(1)}, u32[]{:S(2)}, u32[]{:S(2)}) %collective-permute-start) | collective-permute-done | bytes 25632 | tf_op jit(solution)/shard_map/ppermute | solution.py:105
  17.2 4.4 %collective-permute-start.3 = (f32[1,1,6400]{2,1,0:T(1,128)S(1)}, f32[1,1,6400]{2,1,0:T(1,128)S(1)}, u32[]{:S(2)}, u32[]{:S(2)}) collective-permute-start(f32[1,1,6400]{2,1,0:T(1,128)S(1)} %collective-permute-done.1), channel_id=1, source_target_pairs={{0,30},{2,0},{4,2},{6,4},{8,6},{10,8},{12,10},{14,12},{16,14},{18,... | collective-permute-start | bytes 76808 | tf_op jit(solution)/shard_map/ppermute | solution.py:110
  25.5 4.5 %collective-permute-start.5 = (f32[1,1,6400]{2,1,0:T(1,128)S(1)}, f32[1,1,6400]{2,1,0:T(1,128)S(1)}, u32[]{:S(2)}, u32[]{:S(2)}) collective-permute-start(f32[1,1,6400]{2,1,0:T(1,128)S(1)} %collective-permute-done.3), channel_id=1, source_target_pairs={{0,30},{2,0},{4,2},{6,4},{8,6},{10,8},{12,10},{14,12},{16,14},{18,... | collective-permute-start | bytes 76808 | tf_op jit(solution)/shard_map/ppermute | solution.py:110
  31.5 4.4 %collective-permute-start.7 = (f32[1,1,6400]{2,1,0:T(1,128)S(1)}, f32[1,1,6400]{2,1,0:T(1,128)S(1)}, u32[]{:S(2)}, u32[]{:S(2)}) collective-permute-start(f32[1,1,6400]{2,1,0:T(1,128)S(1)} %collective-permute-done.5), channel_id=1, source_target_pairs={{0,30},{2,0},{4,2},{6,4},{8,6},{10,8},{12,10},{14,12},{16,14},{18,... | collective-permute-start | bytes 76808 | tf_op jit(solution)/shard_map/ppermute | solution.py:110
  37.4 4.4 %collective-permute-start.9 = (f32[1,1,6400]{2,1,0:T(1,128)S(1)}, f32[1,1,6400]{2,1,0:T(1,128)S(1)}, u32[]{:S(2)}, u32[]{:S(2)}) collective-permute-start(f32[1,1,6400]{2,1,0:T(1,128)S(1)} %collective-permute-done.7), channel_id=1, source_target_pairs={{0,30},{2,0},{4,2},{6,4},{8,6},{10,8},{12,10},{14,12},{16,14},{18,... | collective-permute-start | bytes 76808 | tf_op jit(solution)/shard_map/ppermute | solution.py:110
  43.5 4.5 %collective-permute-start.11 = (f32[1,1,6400]{2,1,0:T(1,128)S(1)}, f32[1,1,6400]{2,1,0:T(1,128)S(1)}, u32[]{:S(2)}, u32[]{:S(2)}) collective-permute-start(f32[1,1,6400]{2,1,0:T(1,128)S(1)} %collective-permute-done.9), channel_id=1, source_target_pairs={{0,30},{2,0},{4,2},{6,4},{8,6},{10,8},{12,10},{14,12},{16,14},{18,... | collective-permute-start | bytes 76808 | tf_op jit(solution)/shard_map/ppermute | solution.py:110
  49.5 4.5 %collective-permute-start.13 = (f32[1,1,6400]{2,1,0:T(1,128)S(1)}, f32[1,1,6400]{2,1,0:T(1,128)S(1)}, u32[]{:S(2)}, u32[]{:S(2)}) collective-permute-start(f32[1,1,6400]{2,1,0:T(1,128)S(1)} %collective-permute-done.11), channel_id=1, source_target_pairs={{0,30},{2,0},{4,2},{6,4},{8,6},{10,8},{12,10},{14,12},{16,14},{18,... | collective-permute-start | bytes 76808 | tf_op jit(solution)/shard_map/ppermute | solution.py:110
  80.2 13.9 %collective-permute-done.17 = bf16[3,30,4096]{2,1,0:T(8,128)(2,1)S(1)} collective-permute-done((bf16[3,30,4096]{2,1,0:T(8,128)(2,1)S(1)}, bf16[3,30,4096]{2,1,0:T(8,128)(2,1)S(1)}, u32[]{:S(2)}, u32[]{:S(2)}) %collective-permute-start.17) | collective-permute-done | bytes 737312 | tf_op jit(solution)/shard_map/ppermute | solution.py:28
  94.2 9.1 %while.35 = (s32[]{:T(128)}, f32[3,2048]{1,0:T(4,128)S(1)}, f32[3,2048]{1,0:T(4,128)S(1)}, bf16[3,30,2048]{2,1,0:T(8,128)(2,1)S(1)}, bf16[3,30,2048]{2,1,0:T(8,128)(2,1)S(1)}, /*index=5*/s32[]{:T(128)}, s32[]{:T(128)}) while((s32[]{:T(128)}, f32[3,2048]{1,0:T(4,128)S(1)}, f32[3,2048]{1,0:T(4,128)S(1)}, bf16[3,30,2048]{2,1,0:T(8,128)(2,1)S(1)}, ...), condition=%wide.region_18.19_spmd, body=%wide.region_13.18_spmd.sunk | while | flops 272627712 | bytes 737377 | solution.py:82
  103.3 9.2 %while.36 = (s32[]{:T(128)}, f32[3,2048]{1,0:T(4,128)S(1)}, f32[3,2048]{1,0:T(4,128)S(1)}, bf16[3,30,2048]{2,1,0:T(8,128)(2,1)S(1)}, bf16[3,30,2048]{2,1,0:T(8,128)(2,1)S(1)}, /*index=5*/s32[]{:T(128)}, s32[]{:T(128)}) while((s32[]{:T(128)}, f32[3,2048]{1,0:T(4,128)S(1)}, f32[3,2048]{1,0:T(4,128)S(1)}, bf16[3,30,2048]{2,1,0:T(8,128)(2,1)S(1)}, ...), condition=%wide.region_24.25_spmd, body=%wide.region_19.24_spmd.sunk | while | flops 272627712 | bytes 737377 | solution.py:82
  114.2 30.6 %while.34 = (s32[]{:T(128)}, f32[3,4096]{1,0:T(4,128)S(1)}, bf16[3,30,4096]{2,1,0:T(8,128)(2,1)S(1)}, s32[]{:T(128)}, s32[]{:T(128)}) while((s32[]{:T(128)}, f32[3,4096]{1,0:T(4,128)S(1)}, bf16[3,30,4096]{2,1,0:T(8,128)(2,1)S(1)}, s32[]{:T(128)}, s32[]{:T(128)}) %tuple.68), condition=%wide.region_12.13_spmd, body=%wide.region_7.12_spmd.sunk | while | flops 1073750016 | bytes 1884229 | solution.py:65
  114.4 2.5 %convert_reduce_fusion.20 = f32[1024]{0:T(1024)S(1)} fusion(bf16[30,4096]{1,0:T(8,128)(2,1)S(1)} %dynamic-slice_bitcast_fusion.6), kind=kOutput, calls=%fused_computation.clone.1 | convolution fusion | flops 268434432 | bytes 331776 | tf_op jit(solution)/shard_map/while/body/eval_jaxpr/dot_general | solution.py:44
  116.9 2.4 %convert_reduce_fusion.21 = f32[1024]{0:T(1024)S(1)} fusion(bf16[30,4096]{1,0:T(8,128)(2,1)S(1)} %dynamic-slice_bitcast_fusion.6), kind=kOutput, calls=%fused_computation.1.clone.1 | convolution fusion | flops 268434432 | bytes 331776 | tf_op jit(solution)/shard_map/while/body/eval_jaxpr/dot_general | solution.py:44
  119.3 2.4 %convert_reduce_fusion.22 = f32[1024]{0:T(1024)S(1)} fusion(bf16[30,4096]{1,0:T(8,128)(2,1)S(1)} %dynamic-slice_bitcast_fusion.6), kind=kOutput, calls=%fused_computation.2.clone.1 | convolution fusion | flops 268434432 | bytes 331776 | tf_op jit(solution)/shard_map/while/body/eval_jaxpr/dot_general | solution.py:44
  121.8 2.5 %convert_reduce_fusion.23 = f32[1024]{0:T(1024)S(1)} fusion(bf16[30,4096]{1,0:T(8,128)(2,1)S(1)} %dynamic-slice_bitcast_fusion.6), kind=kOutput, calls=%fused_computation.3.clone.1 | convolution fusion | flops 268434432 | bytes 331776 | tf_op jit(solution)/shard_map/while/body/eval_jaxpr/dot_general | solution.py:44
  124.6 2.4 %convert_reduce_fusion.20 = f32[1024]{0:T(1024)S(1)} fusion(bf16[30,4096]{1,0:T(8,128)(2,1)S(1)} %dynamic-slice_bitcast_fusion.6), kind=kOutput, calls=%fused_computation.clone.1 | convolution fusion | flops 268434432 | bytes 331776 | tf_op jit(solution)/shard_map/while/body/eval_jaxpr/dot_general | solution.py:44
  127.0 2.5 %convert_reduce_fusion.21 = f32[1024]{0:T(1024)S(1)} fusion(bf16[30,4096]{1,0:T(8,128)(2,1)S(1)} %dynamic-slice_bitcast_fusion.6), kind=kOutput, calls=%fused_computation.1.clone.1 | convolution fusion | flops 268434432 | bytes 331776 | tf_op jit(solution)/shard_map/while/body/eval_jaxpr/dot_general | solution.py:44
  129.5 2.5 %convert_reduce_fusion.22 = f32[1024]{0:T(1024)S(1)} fusion(bf16[30,4096]{1,0:T(8,128)(2,1)S(1)} %dynamic-slice_bitcast_fusion.6), kind=kOutput, calls=%fused_computation.2.clone.1 | convolution fusion | flops 268434432 | bytes 331776 | tf_op jit(solution)/shard_map/while/body/eval_jaxpr/dot_general | solution.py:44
  131.9 2.5 %convert_reduce_fusion.23 = f32[1024]{0:T(1024)S(1)} fusion(bf16[30,4096]{1,0:T(8,128)(2,1)S(1)} %dynamic-slice_bitcast_fusion.6), kind=kOutput, calls=%fused_computation.3.clone.1 | convolution fusion | flops 268434432 | bytes 331776 | tf_op jit(solution)/shard_map/while/body/eval_jaxpr/dot_general | solution.py:44
  137.1 2.5 %convert_reduce_fusion.21 = f32[1024]{0:T(1024)S(1)} fusion(bf16[30,4096]{1,0:T(8,128)(2,1)S(1)} %dynamic-slice_bitcast_fusion.6), kind=kOutput, calls=%fused_computation.1.clone.1 | convolution fusion | flops 268434432 | bytes 331776 | tf_op jit(solution)/shard_map/while/body/eval_jaxpr/dot_general | solution.py:44
  139.6 2.5 %convert_reduce_fusion.22 = f32[1024]{0:T(1024)S(1)} fusion(bf16[30,4096]{1,0:T(8,128)(2,1)S(1)} %dynamic-slice_bitcast_fusion.6), kind=kOutput, calls=%fused_computation.2.clone.1 | convolution fusion | flops 268434432 | bytes 331776 | tf_op jit(solution)/shard_map/while/body/eval_jaxpr/dot_general | solution.py:44
  142.0 2.5 %convert_reduce_fusion.23 = f32[1024]{0:T(1024)S(1)} fusion(bf16[30,4096]{1,0:T(8,128)(2,1)S(1)} %dynamic-slice_bitcast_fusion.6), kind=kOutput, calls=%fused_computation.3.clone.1 | convolution fusion | flops 268434432 | bytes 331776 | tf_op jit(solution)/shard_map/while/body/eval_jaxpr/dot_general | solution.py:44
  (149 shorter events, 59.6 us)
Async XLA Ops:
  0.0 23.1 %all-to-all-start = ((f32[16,1,3840]{2,1,0:T(1,128)}), f32[16,1,3840]{2,1,0:T(1,128)S(1)}, u32[]{:S(2)}, u32[]{:S(2)}) async-start(f32[16,1,3840]{2,1,0:T(1,128)} %bitcast.92), calls=%async_computation | async-start | bytes 491520 | tf_op jit(solution)/shard_map/all_to_all | solution.py:93
  7.4 9.7 %collective-permute-start = (f32[1,1,6400]{2,1,0:T(1,128)}, f32[1,1,6400]{2,1,0:T(1,128)S(1)}, u32[]{:S(2)}, u32[]{:S(2)}) collective-permute-start(f32[1,1,6400]{2,1,0:T(1,128)} %param.9), channel_id=1, source_target_pairs={{0,2},{2,4},{4,6},{6,8},{8,10},{10,12},{12,14},{14,16},{16,18},{18... | collective-permute-start | bytes 76808 | tf_op jit(solution)/shard_map/ppermute | solution.py:105
  7.8 9.3 %collective-permute-start.1 = (f32[1,1,6400]{2,1,0:T(1,128)}, f32[1,1,6400]{2,1,0:T(1,128)S(1)}, u32[]{:S(2)}, u32[]{:S(2)}) collective-permute-start(f32[1,1,6400]{2,1,0:T(1,128)} %param.9), channel_id=1, source_target_pairs={{0,30},{2,0},{4,2},{6,4},{8,6},{10,8},{12,10},{14,12},{16,14},{18,... | collective-permute-start | bytes 76808 | tf_op jit(solution)/shard_map/ppermute | solution.py:110
  17.2 6.0 %collective-permute-start.2 = (f32[1,1,6400]{2,1,0:T(1,128)S(1)}, f32[1,1,6400]{2,1,0:T(1,128)S(1)}, u32[]{:S(2)}, u32[]{:S(2)}) collective-permute-start(f32[1,1,6400]{2,1,0:T(1,128)S(1)} %collective-permute-done), channel_id=1, source_target_pairs={{0,2},{2,4},{4,6},{6,8},{8,10},{10,12},{12,14},{14,16},{16,18},{18... | collective-permute-start | bytes 76808 | tf_op jit(solution)/shard_map/ppermute | solution.py:105
  17.2 8.3 %collective-permute-start.3 = (f32[1,1,6400]{2,1,0:T(1,128)S(1)}, f32[1,1,6400]{2,1,0:T(1,128)S(1)}, u32[]{:S(2)}, u32[]{:S(2)}) collective-permute-start(f32[1,1,6400]{2,1,0:T(1,128)S(1)} %collective-permute-done.1), channel_id=1, source_target_pairs={{0,30},{2,0},{4,2},{6,4},{8,6},{10,8},{12,10},{14,12},{16,14},{18,... | collective-permute-start | bytes 76808 | tf_op jit(solution)/shard_map/ppermute | solution.py:110
  23.1 6.8 %collective-permute-start.4 = (f32[1,1,6400]{2,1,0:T(1,128)S(1)}, f32[1,1,6400]{2,1,0:T(1,128)S(1)}, u32[]{:S(2)}, u32[]{:S(2)}) collective-permute-start(f32[1,1,6400]{2,1,0:T(1,128)S(1)} %collective-permute-done.2), channel_id=1, source_target_pairs={{0,2},{2,4},{4,6},{6,8},{8,10},{10,12},{12,14},{14,16},{16,18},{18... | collective-permute-start | bytes 76808 | tf_op jit(solution)/shard_map/ppermute | solution.py:105
  23.7 30.7 %copy-start.1 = (f32[1,1,6400]{2,1,0:T(1,128)S(1)}, f32[1,1,6400]{2,1,0:T(1,128)}, u32[]{:S(2)}) copy-start(f32[1,1,6400]{2,1,0:T(1,128)} %param.9) | copy-start | bytes 76804
  24.2 41.2 %collective-permute-start.16 = (f32[15,4096]{1,0:T(8,128)S(1)}, f32[15,4096]{1,0:T(8,128)S(1)}, u32[]{:S(2)}, u32[]{:S(2)}) collective-permute-start(f32[15,4096]{1,0:T(8,128)S(1)} %bitcast.85), channel_id=1, source_target_pairs={{0,2},{2,4},{4,6},{6,8},{8,10},{10,12},{12,14},{14,16},{16,18},{18... | collective-permute-start | bytes 737288 | tf_op jit(solution)/shard_map/ppermute | solution.py:18
  25.5 6.0 %collective-permute-start.5 = (f32[1,1,6400]{2,1,0:T(1,128)S(1)}, f32[1,1,6400]{2,1,0:T(1,128)S(1)}, u32[]{:S(2)}, u32[]{:S(2)}) collective-permute-start(f32[1,1,6400]{2,1,0:T(1,128)S(1)} %collective-permute-done.3), channel_id=1, source_target_pairs={{0,30},{2,0},{4,2},{6,4},{8,6},{10,8},{12,10},{14,12},{16,14},{18,... | collective-permute-start | bytes 76808 | tf_op jit(solution)/shard_map/ppermute | solution.py:110
  30.0 6.0 %collective-permute-start.6 = (f32[1,1,6400]{2,1,0:T(1,128)S(1)}, f32[1,1,6400]{2,1,0:T(1,128)S(1)}, u32[]{:S(2)}, u32[]{:S(2)}) collective-permute-start(f32[1,1,6400]{2,1,0:T(1,128)S(1)} %collective-permute-done.4), channel_id=1, source_target_pairs={{0,2},{2,4},{4,6},{6,8},{8,10},{10,12},{12,14},{14,16},{16,18},{18... | collective-permute-start | bytes 76808 | tf_op jit(solution)/shard_map/ppermute | solution.py:105
  31.5 6.0 %collective-permute-start.7 = (f32[1,1,6400]{2,1,0:T(1,128)S(1)}, f32[1,1,6400]{2,1,0:T(1,128)S(1)}, u32[]{:S(2)}, u32[]{:S(2)}) collective-permute-start(f32[1,1,6400]{2,1,0:T(1,128)S(1)} %collective-permute-done.5), channel_id=1, source_target_pairs={{0,30},{2,0},{4,2},{6,4},{8,6},{10,8},{12,10},{14,12},{16,14},{18,... | collective-permute-start | bytes 76808 | tf_op jit(solution)/shard_map/ppermute | solution.py:110
  35.9 6.0 %collective-permute-start.8 = (f32[1,1,6400]{2,1,0:T(1,128)S(1)}, f32[1,1,6400]{2,1,0:T(1,128)S(1)}, u32[]{:S(2)}, u32[]{:S(2)}) collective-permute-start(f32[1,1,6400]{2,1,0:T(1,128)S(1)} %collective-permute-done.6), channel_id=1, source_target_pairs={{0,2},{2,4},{4,6},{6,8},{8,10},{10,12},{12,14},{14,16},{16,18},{18... | collective-permute-start | bytes 76808 | tf_op jit(solution)/shard_map/ppermute | solution.py:105
  37.4 6.1 %collective-permute-start.9 = (f32[1,1,6400]{2,1,0:T(1,128)S(1)}, f32[1,1,6400]{2,1,0:T(1,128)S(1)}, u32[]{:S(2)}, u32[]{:S(2)}) collective-permute-start(f32[1,1,6400]{2,1,0:T(1,128)S(1)} %collective-permute-done.7), channel_id=1, source_target_pairs={{0,30},{2,0},{4,2},{6,4},{8,6},{10,8},{12,10},{14,12},{16,14},{18,... | collective-permute-start | bytes 76808 | tf_op jit(solution)/shard_map/ppermute | solution.py:110
  41.9 6.1 %collective-permute-start.10 = (f32[1,1,6400]{2,1,0:T(1,128)S(1)}, f32[1,1,6400]{2,1,0:T(1,128)S(1)}, u32[]{:S(2)}, u32[]{:S(2)}) collective-permute-start(f32[1,1,6400]{2,1,0:T(1,128)S(1)} %collective-permute-done.8), channel_id=1, source_target_pairs={{0,2},{2,4},{4,6},{6,8},{8,10},{10,12},{12,14},{14,16},{16,18},{18... | collective-permute-start | bytes 76808 | tf_op jit(solution)/shard_map/ppermute | solution.py:105
  42.2 23.2 %collective-permute-start.15 = (f32[10,4096]{1,0:T(8,128)S(1)}, f32[10,4096]{1,0:T(8,128)S(1)}, u32[]{:S(2)}, u32[]{:S(2)}) collective-permute-start(f32[10,4096]{1,0:T(8,128)S(1)} %bitcast.91), channel_id=1, source_target_pairs={{0,4},{2,6},{4,8},{6,10},{8,12},{10,14},{12,16},{14,18},{16,20},{1... | collective-permute-start | bytes 491528 | tf_op jit(solution)/shard_map/ppermute | solution.py:18
  43.5 6.0 %collective-permute-start.11 = (f32[1,1,6400]{2,1,0:T(1,128)S(1)}, f32[1,1,6400]{2,1,0:T(1,128)S(1)}, u32[]{:S(2)}, u32[]{:S(2)}) collective-permute-start(f32[1,1,6400]{2,1,0:T(1,128)S(1)} %collective-permute-done.9), channel_id=1, source_target_pairs={{0,30},{2,0},{4,2},{6,4},{8,6},{10,8},{12,10},{14,12},{16,14},{18,... | collective-permute-start | bytes 76808 | tf_op jit(solution)/shard_map/ppermute | solution.py:110
  48.0 6.1 %collective-permute-start.12 = (f32[1,1,6400]{2,1,0:T(1,128)S(1)}, f32[1,1,6400]{2,1,0:T(1,128)S(1)}, u32[]{:S(2)}, u32[]{:S(2)}) collective-permute-start(f32[1,1,6400]{2,1,0:T(1,128)S(1)} %collective-permute-done.10), channel_id=1, source_target_pairs={{0,2},{2,4},{4,6},{6,8},{8,10},{10,12},{12,14},{14,16},{16,18},{18... | collective-permute-start | bytes 76808 | tf_op jit(solution)/shard_map/ppermute | solution.py:105
  49.5 13.6 %collective-permute-start.13 = (f32[1,1,6400]{2,1,0:T(1,128)S(1)}, f32[1,1,6400]{2,1,0:T(1,128)S(1)}, u32[]{:S(2)}, u32[]{:S(2)}) collective-permute-start(f32[1,1,6400]{2,1,0:T(1,128)S(1)} %collective-permute-done.11), channel_id=1, source_target_pairs={{0,30},{2,0},{4,2},{6,4},{8,6},{10,8},{12,10},{14,12},{16,14},{18,... | collective-permute-start | bytes 76808 | tf_op jit(solution)/shard_map/ppermute | solution.py:110
  54.1 9.7 %collective-permute-start.14 = (f32[1,1,6400]{2,1,0:T(1,128)S(1)}, f32[1,1,6400]{2,1,0:T(1,128)S(1)}, u32[]{:S(2)}, u32[]{:S(2)}) collective-permute-start(f32[1,1,6400]{2,1,0:T(1,128)S(1)} %collective-permute-done.12), channel_id=1, source_target_pairs={{0,2},{2,4},{4,6},{6,8},{8,10},{10,12},{12,14},{14,16},{16,18},{18... | collective-permute-start | bytes 76808 | tf_op jit(solution)/shard_map/ppermute | solution.py:105
  74.6 1.6 %copy-start = (f32[3,4096]{1,0:T(4,128)S(1)}, f32[3,4096]{1,0:T(4,128)}, u32[]{:S(2)}) copy-start(f32[3,4096]{1,0:T(4,128)} %get-tuple-element.128) | copy-start | bytes 147460
  78.6 15.5 %collective-permute-start.17 = (bf16[3,30,4096]{2,1,0:T(8,128)(2,1)S(1)}, bf16[3,30,4096]{2,1,0:T(8,128)(2,1)S(1)}, u32[]{:S(2)}, u32[]{:S(2)}) collective-permute-start(bf16[3,30,4096]{2,1,0:T(8,128)(2,1)S(1)} %multiply_convert_fusion), channel_id=1, source_target_pairs={{0,1},{1,0},{2,3},{3,2},{4,5},{5,4},{6,7},{7,6},{8,9},{9,8},{10,11... | collective-permute-start | bytes 2211848 | tf_op jit(solution)/shard_map/ppermute | solution.py:28
  112.6 32.2 %collective-permute-start.18 = (bf16[3,4096]{1,0:T(4,128)(2,1)S(1)}, bf16[3,4096]{1,0:T(4,128)(2,1)S(1)}, u32[]{:S(2)}, u32[]{:S(2)}) collective-permute-start(bf16[3,4096]{1,0:T(4,128)(2,1)S(1)} %convert_element_type.58), channel_id=1, source_target_pairs={{0,1},{1,0},{2,3},{3,2},{4,5},{5,4},{6,7},{7,6},{8,9},{9,8},{10,11... | collective-permute-start | bytes 73736 | tf_op jit(solution)/shard_map/ppermute | solution.py:28
